TPU v7x, 32 devices: a whole 2x2x4 slice. The times are simulated.
32 devices in a mesh: shard: 32 (over z, y, x, core).
Axes of the slice: x: 2, y: 2, z: 4, core: 2. Of those that a mesh axis runs over, the one named last changes fastest.
Arguments:
- lookup_ids: int32 [8192, 4, 8], P('shard'), may hold values from 0 to 131071, as said below
- bag_lengths: int32 [8192, 4], P('shard'), may hold values from 1 to 8
- pooled_gradients: bfloat16 [8192, 4, 128], P('shard'), may hold values from -6 to 6
- tables: float32 [4, 131072, 128], P(None, 'shard'), may hold values from -4 to 4
- accumulators: float32 [4, 131072], P(None, 'shard'), may hold values from 0.05 to 2
Outputs:
- new_tables: float32 [4, 131072, 128], P(None, 'shard')
- new_accumulators: float32 [4, 131072], P(None, 'shard')
- gradient_scale: float32 [], replicated
Inputs may be any that keep to these rules, and one draw needn't show every extreme that they name: `lookup_ids`: row ids are rows 0 to 131071 of their table. Among the 256 x 8 entries of one table held by one device (padding positions included), the rows of every owning device's block of 4096 rows are named exactly 64 times. About half the lookups fall on the first 32 rows of an owner's block.
All inputs are finite; a program needn't handle non-finite values.
Results may differ from a plain program's by a relative error of at most 0.0003.
Values may be sent and summed in bfloat16 or wider, within the bound.
A program may use at most 128 MiB of HBM per device.

v0:
```python
import functools

import jax
import jax.numpy as jnp
from jax import lax
from jax.experimental import pallas as pl
from jax.experimental.pallas import tpu as pltpu
from jax.sharding import PartitionSpec as P

step_size = 0.5
epsilon = 1e-08
MESH = pl.DeviceIdType.MESH
NT_DIMS = (((1,), (1,)), ((), ()))
DIGIT = 64


def arrange_kernel(peers, bucket, rows_dev, ids_ref, enc_ref, scaled_ref, terms_ref, rows_ref):
    count_tables, bag_width, samples = ids_ref.shape
    f32, bf16 = jnp.float32, jnp.bfloat16
    tri = (
        lax.broadcasted_iota(jnp.int32, (samples, samples), 0)
        < lax.broadcasted_iota(jnp.int32, (samples, samples), 1)
    ).astype(f32).astype(bf16)
    for t in range(count_tables):
        running = jnp.zeros((peers, 1), f32)
        info_t = jnp.zeros((bucket, peers), f32)
        high = jnp.zeros((peers, bucket), f32)
        low = jnp.zeros((peers, bucket), f32)
        for l in range(bag_width):
            ids = ids_ref[t, l : l + 1, :]
            owner = ids // rows_dev
            local = ids - owner * rows_dev
            hi = local // DIGIT
            lo = local - hi * DIGIT
            own = (lax.broadcasted_iota(jnp.int32, (peers, samples), 0) == owner).astype(f32)
            own_b = own.astype(bf16)
            before = jnp.dot(own_b, tri, preferred_element_type=f32) + running
            rank = jnp.sum(before * own, axis=0, keepdims=True).astype(jnp.int32)
            running = running + jnp.sum(own, axis=1, keepdims=True)
            at_rank = (
                (lax.broadcasted_iota(jnp.int32, (bucket, samples), 0) == rank)
                .astype(f32)
                .astype(bf16)
            )
            enc = enc_ref[t, l : l + 1, :].astype(f32)
            info_t += lax.dot_general(
                at_rank, (own * enc).astype(bf16), NT_DIMS, preferred_element_type=f32
            )
            high += lax.dot_general(
                (own * hi.astype(f32)).astype(bf16), at_rank, NT_DIMS, preferred_element_type=f32
            )
            low += lax.dot_general(
                (own * lo.astype(f32)).astype(bf16), at_rank, NT_DIMS, preferred_element_type=f32
            )
        rows_ref[:, t, :] = (high * DIGIT + low).astype(jnp.int32)
        info_i = info_t.astype(jnp.int32)
        lane = lax.broadcasted_iota(jnp.int32, (bucket, samples), 1)
        group = min(peers, 8)
        for g in range(0, peers, group):
            pick = jnp.concatenate(
                [
                    (lane == info_i[:, o : o + 1]).astype(f32).astype(bf16)
                    for o in range(g, g + group)
                ],
                axis=0,
            )
            moved = jnp.dot(pick, scaled_ref[t], preferred_element_type=f32).astype(bf16)
            for o in range(group):
                terms_ref[g + o, t * bucket : (t + 1) * bucket, :] = moved[
                    o * bucket : (o + 1) * bucket
                ]


def exchange_kernel(n, terms_ref, rows_ref, got_ref, got_rows_ref, send, recv, rsend, rrecv, local):
    me = lax.axis_index("shard")
    barrier = pltpu.get_barrier_semaphore()

    @pl.loop(1, n)
    def _(i):
        pl.semaphore_signal(
            barrier, inc=1, device_id=(lax.rem(me + i, n),), device_id_type=MESH
        )

    own = pltpu.make_async_copy(terms_ref.at[me], got_ref.at[0], local.at[0])
    own.start()
    own_rows = pltpu.make_async_copy(rows_ref.at[me], got_rows_ref.at[0], local.at[1])
    own_rows.start()
    pl.semaphore_wait(barrier, n - 1)

    def copies(i):
        peer = lax.rem(me + i, n)
        return (
            pltpu.make_async_remote_copy(
                src_ref=rows_ref.at[peer],
                dst_ref=got_rows_ref.at[i],
                send_sem=rsend.at[i],
                recv_sem=rrecv.at[i],
                device_id=(peer,),
                device_id_type=MESH,
            ),
            pltpu.make_async_remote_copy(
                src_ref=terms_ref.at[peer],
                dst_ref=got_ref.at[i],
                send_sem=send.at[i],
                recv_sem=recv.at[i],
                device_id=(peer,),
                device_id_type=MESH,
            ),
        )

    @pl.loop(1, n)
    def _(i):
        for copy in copies(i):
            copy.start()

    own.wait()
    own_rows.wait()

    @pl.loop(1, n)
    def _(i):
        for copy in copies(i):
            copy.wait()


def update_kernel(parts, rows_ref, terms_ref, tables_ref, accum_ref, new_t_ref, new_a_ref, sq_ref):
    f32, bf16 = jnp.float32, jnp.bfloat16
    peers, bucket, width = terms_ref.shape
    count = peers * bucket
    part_rows = tables_ref.shape[2]
    rows = rows_ref[0]
    part = rows // part_rows
    within = rows - part * part_rows
    terms = terms_ref[...].reshape(count, width)
    part_f = part.astype(f32)
    columns = []
    for c in range(0, count, 128):
        columns.append(jnp.broadcast_to(part_f[:, c : c + 128], (128, 128)).T)
    part_col = jnp.concatenate(columns, axis=0)
    wide = jnp.concatenate(
        [
            jnp.where(part_col == q, terms.astype(f32), 0.0).astype(bf16)
            for q in range(parts)
        ],
        axis=1,
    )
    chunk = min(512, part_rows)
    total = jnp.zeros((8, width), f32)
    for m in range(0, part_rows, chunk):
        hot = (
            (lax.broadcasted_iota(jnp.int32, (chunk, count), 0) + m == within)
            .astype(f32)
            .astype(bf16)
        )
        summed = jnp.dot(hot, wide, preferred_element_type=f32)
        for q in range(parts):
            for r in range(0, chunk, 128):
                s = summed[r : r + 128, q * width : (q + 1) * width]
                square = s * s
                total += jnp.sum(square.reshape(16, 8, width), axis=0)
                mean = jnp.sum(square.T, axis=0, keepdims=True) * (1.0 / width)
                line = (m + r) // 128
                new_a = accum_ref[0, q, line : line + 1, :] + mean
                new_a_ref[0, q, line : line + 1, :] = new_a
                factor = step_size / (jnp.sqrt(new_a) + epsilon)
                spread = jnp.broadcast_to(factor, (128, 128)).T
                new_t_ref[0, q, m + r : m + r + 128, :] = (
                    tables_ref[0, q, m + r : m + r + 128, :] - s * spread
                )

    @pl.when(pl.program_id(0) == 0)
    def _():
        sq_ref[...] = jnp.zeros_like(sq_ref)

    sq_ref[...] += total


def scale_kernel(n, inverse, sq_ref, out_ref, got, send, recv):
    me = lax.axis_index("shard")
    barrier = pltpu.get_barrier_semaphore()

    @pl.loop(1, n)
    def _(i):
        pl.semaphore_signal(
            barrier, inc=1, device_id=(lax.rem(me + i, n),), device_id_type=MESH
        )

    pl.semaphore_wait(barrier, n - 1)

    def copy(i):
        peer = lax.rem(me + i, n)
        return pltpu.make_async_remote_copy(
            src_ref=sq_ref,
            dst_ref=got.at[i],
            send_sem=send.at[i],
            recv_sem=recv.at[i],
            device_id=(peer,),
            device_id_type=MESH,
        )

    @pl.loop(1, n)
    def _(i):
        copy(i).start()

    @pl.loop(1, n)
    def _(i):
        copy(i).wait()

    total = sq_ref[...] + jnp.sum(got[1:], axis=0)
    value = jnp.sum(jnp.sum(total, axis=1, keepdims=True), axis=0, keepdims=True)
    out_ref[...] = jnp.broadcast_to(jnp.sqrt(value * inverse), out_ref.shape)


def on_device(lookup_ids, bag_lengths, pooled_gradients, tables, accumulators):
    samples, count_tables, bag_width = lookup_ids.shape
    width = pooled_gradients.shape[2]
    rows_dev = tables.shape[1]
    n = lax.axis_size("shard")
    lookups = samples * bag_width
    bucket = lookups // n
    vmem = pl.BlockSpec(memory_space=pltpu.VMEM)
    anywhere = pl.BlockSpec(memory_space=pl.ANY)
    assert samples <= 256 and rows_dev <= 256 * DIGIT

    ids = lookup_ids.transpose(1, 2, 0)
    position = jnp.arange(bag_width, dtype=jnp.int32)
    sample = jnp.arange(samples, dtype=jnp.int32)
    inside = position[None, :, None] < bag_lengths.T[:, None, :]
    enc = jnp.where(inside, sample[None, None, :], -1)
    scaled = (
        (pooled_gradients.astype(jnp.float32) / bag_lengths[:, :, None].astype(jnp.float32))
        .astype(jnp.bfloat16)
        .transpose(1, 0, 2)
    )
    send_terms, send_rows = pl.pallas_call(
        functools.partial(arrange_kernel, n, bucket, rows_dev),
        out_shape=(
            jax.ShapeDtypeStruct((n, count_tables * bucket, width), jnp.bfloat16),
            jax.ShapeDtypeStruct((n, count_tables, bucket), jnp.int32),
        ),
        in_specs=[vmem] * 3,
        out_specs=(vmem, vmem),
    )(ids, enc, scaled)

    dma = pltpu.SemaphoreType.DMA
    got_terms, got_rows = pl.pallas_call(
        functools.partial(exchange_kernel, n),
        out_shape=(
            jax.ShapeDtypeStruct(send_terms.shape, jnp.bfloat16),
            jax.ShapeDtypeStruct(send_rows.shape, jnp.int32),
        ),
        in_specs=[vmem, vmem],
        out_specs=(vmem, vmem),
        scratch_shapes=[dma((n,)), dma((n,)), dma((n,)), dma((n,)), dma((2,))],
        compiler_params=pltpu.CompilerParams(collective_id=0, has_side_effects=True),
    )(send_terms, send_rows)
    table_rows = got_rows.transpose(1, 0, 2).reshape(count_tables, 1, lookups)

    parts = 4
    part_rows = rows_dev // parts
    lines = part_rows // 128
    new_tables, new_accumulators, squares = pl.pallas_call(
        functools.partial(update_kernel, parts),
        grid=(count_tables,),
        out_shape=(
            jax.ShapeDtypeStruct((count_tables, parts, part_rows, width), jnp.float32),
            jax.ShapeDtypeStruct((count_tables, parts, lines, 128), jnp.float32),
            jax.ShapeDtypeStruct((8, width), jnp.float32),
        ),
        in_specs=[
            pl.BlockSpec((1, 1, lookups), lambda t: (t, 0, 0)),
            pl.BlockSpec((n, bucket, width), lambda t: (0, t, 0)),
            pl.BlockSpec((1, parts, part_rows, width), lambda t: (t, 0, 0, 0)),
            pl.BlockSpec((1, parts, lines, 128), lambda t: (t, 0, 0, 0)),
        ],
        out_specs=(
            pl.BlockSpec((1, parts, part_rows, width), lambda t: (t, 0, 0, 0)),
            pl.BlockSpec((1, parts, lines, 128), lambda t: (t, 0, 0, 0)),
            pl.BlockSpec((8, width), lambda t: (0, 0)),
        ),
        compiler_params=pltpu.CompilerParams(vmem_limit_bytes=48 * 1024 * 1024),
    )(
        table_rows,
        got_terms,
        tables.reshape(count_tables, parts, part_rows, width),
        accumulators.reshape(count_tables, parts, lines, 128),
    )

    lookup_count = width * count_tables * lookups * n
    scale = pl.pallas_call(
        functools.partial(scale_kernel, n, 1.0 / lookup_count),
        out_shape=jax.ShapeDtypeStruct((8, 128), jnp.float32),
        in_specs=[vmem],
        out_specs=vmem,
        scratch_shapes=[
            pltpu.VMEM((n, 8, width), jnp.float32),
            dma((n,)),
            dma((n,)),
        ],
        compiler_params=pltpu.CompilerParams(collective_id=1, has_side_effects=True),
    )(squares)
    return (
        new_tables.reshape(tables.shape),
        new_accumulators.reshape(accumulators.shape),
        scale[0, 0],
    )


def solution(mesh):
    return jax.shard_map(
        on_device,
        mesh=mesh,
        in_specs=(
            P("shard", None, None),
            P("shard", None),
            P("shard", None, None),
            P(None, "shard", None),
            P(None, "shard"),
        ),
        out_specs=(P(None, "shard", None), P(None, "shard"), P()),
        check_vma=False,
    )
```

profile of v0, /device:TPU:0, one launch (start us, length us, event | category | flops | bytes accessed | tf_op | source)
XLA Modules:
  0.0 106.3 jit_solution(14317088181681076524)
XLA Ops:
  0.6 0.7 convert_element_type.11
  1.3 1.3 %iota_select_fusion.enc_ref = s32[4,8,256]{2,1,0:T(8,128)} fusion(s32[4,256]{1,0:T(4,128)} %bitcast.25), kind=kLoop, calls=%fused_computation.4 | loop fusion | flops 16384 | bytes 36864 | tf_op jit(solution)/shard_map/jit(_where)/select_n | solution.py:228
  2.6 0.8 copy.16
  3.5 1.8 %fusion.scaled_ref = bf16[4,256,128]{2,1,0:T(8,128)(2,1)} fusion(bf16[256,4,128]{2,1,0:T(4,128)(2,1)} %param.7, f32[256,4]{0,1:T(4,128)S(1)} %convert_element_type.11), kind=kLoop, calls=%fused_computation.1 | loop fusion | flops 393216 | bytes 528384 | tf_op jit(solution)/shard_map/transpose | solution.py:232
  5.3 10.0 %shard_map.76 = (bf16[32,256,128]{2,1,0:T(8,128)(2,1)}, s32[32,4,64]{2,1,0:T(4,128)}) custom-call(s32[4,8,256]{2,1,0:T(8,128)} %bitcast.24, s32[4,8,256]{2,1,0:T(8,128)} %iota_select_fusion.enc_ref, bf16[4,256,128]{2,1,0:T(8,128)(2,1)} %fusion.scaled_ref), custom_call_target="tpu_custom_call" | custom-call | tf_op jit(solution)/shard_map/pallas_call | solution.py:234
  15.3 49.3 %shard_map.77 = (bf16[32,256,128]{2,1,0:T(8,128)(2,1)}, s32[32,4,64]{2,1,0:T(4,128)}) custom-call(bf16[32,256,128]{2,1,0:T(8,128)(2,1)} %get-tuple-element.10.terms_ref, s32[32,4,64]{2,1,0:T(4,128)} %get-tuple-element.11.rows_ref), custom_call_target="tpu_custom_call" | custom-call | tf_op jit(solution)/shard_map/pallas_call | solution.py:245
  64.7 0.8 copy.9
  65.5 0.1 reshape.24.rows_ref
  65.6 0.0 copy-start
  65.6 1.6 %copy-done = bf16[32,256,128]{2,1,0:T(8,128)(2,1)S(1)} copy-done((bf16[32,256,128]{2,1,0:T(8,128)(2,1)S(1)}, bf16[32,256,128]{2,1,0:T(8,128)(2,1)}, u32[]{:S(2)}) %copy-start) | copy-done | bytes 2097176
  67.2 15.5 %shard_map.78 = (f32[4,4,1024,128]{3,2,1,0:T(8,128)}, f32[4,4,8,128]{3,2,1,0:T(8,128)S(1)}, f32[8,128]{1,0:T(8,128)S(1)}) custom-call(s32[4,1,2048]{2,1,0:T(1,128)S(1)} %reshape.24.rows_ref, bf16[32,256,128]{2,1,0:T(8,128)(2,1)S(1)} %copy-done, f32[4,4,1024,128]{3,2,1,0:T(8,128)} %bitcast.20, f32[4,4,8,128]{3,2,1,0:T(8,128)S(1)} %bitcast.18), custom_call_target="tpu_custom_call" | custom-call | tf_op jit(solution)/shard_map/pallas_call | solution.py:261
  82.7 0.0 copy-start.1
  82.7 0.7 copy.15
  83.3 0.0 copy-done.1
  83.3 21.8 %shard_map.79 = f32[8,128]{1,0:T(8,128)} custom-call(f32[8,128]{1,0:T(8,128)} %copy-done.1), custom_call_target="tpu_custom_call" | custom-call | tf_op jit(solution)/shard_map/pallas_call | solution.py:289
  105.1 1.2 %slice.3 = f32[1,1]{1,0:T(1,128)} slice(f32[8,128]{1,0:T(8,128)} %shard_map.79), slice={[0:1], [0:1]} | slice | bytes 8 | tf_op jit(solution)/shard_map/slice | solution.py:304
Async XLA Ops:
  65.6 1.6 %copy-start = (bf16[32,256,128]{2,1,0:T(8,128)(2,1)S(1)}, bf16[32,256,128]{2,1,0:T(8,128)(2,1)}, u32[]{:S(2)}) copy-start(bf16[32,256,128]{2,1,0:T(8,128)(2,1)} %get-tuple-element.13.terms_ref) | copy-start | bytes 6291460
  82.7 0.7 copy-start.1
where the time goes:
time: 107 us; the launch traced here: 106 us
  Pallas kernels  96.6 us (90%)
  local copies, waits for them, and re-layouts  5.25 us (5%)
  other arithmetic  3.84 us (4%)
    pallas_call x1, Pallas kernels, on_device(): pl.pallas_call(functools.partial(exchange_kernel, n), out_shape=(jax.Shap...  49.3 us
    pallas_call x1, Pallas kernels, on_device(): pl.pallas_call(functools.partial(scale_kernel, n, 1.0 / lookup_count), ou...  21.8 us
    pallas_call x1, Pallas kernels, on_device(): pl.pallas_call(functools.partial(update_kernel, parts), grid=(count_table...  15.5 us
    pallas_call x1, Pallas kernels, on_device(): pl.pallas_call(functools.partial(arrange_kernel, n, bucket, rows_dev), ou...  10 us
    unnamed x6, local copies, waits for them, and re-layouts  3.1 us

commit v1 on v0

v1 whole, which is shorter than its diff:
```python
import functools

import jax
import jax.numpy as jnp
from jax import lax
from jax.experimental import pallas as pl
from jax.experimental.pallas import tpu as pltpu
from jax.sharding import PartitionSpec as P

step_size = 0.5
epsilon = 1e-08
MESH = pl.DeviceIdType.MESH
NT_DIMS = (((1,), (1,)), ((), ()))
DIGIT = 64


def arrange_kernel(peers, bucket, rows_dev, ids_ref, enc_ref, scaled_ref, terms_ref, rows_ref):
    count_tables, bag_width, samples = ids_ref.shape
    f32, bf16 = jnp.float32, jnp.bfloat16
    tri = (
        lax.broadcasted_iota(jnp.int32, (samples, samples), 0)
        < lax.broadcasted_iota(jnp.int32, (samples, samples), 1)
    ).astype(f32).astype(bf16)
    for t in range(count_tables):
        running = jnp.zeros((peers, 1), f32)
        info_t = jnp.zeros((bucket, peers), f32)
        high = jnp.zeros((peers, bucket), f32)
        low = jnp.zeros((peers, bucket), f32)
        for l in range(bag_width):
            ids = ids_ref[t, l : l + 1, :]
            owner = ids // rows_dev
            local = ids - owner * rows_dev
            hi = local // DIGIT
            lo = local - hi * DIGIT
            own = (lax.broadcasted_iota(jnp.int32, (peers, samples), 0) == owner).astype(f32)
            own_b = own.astype(bf16)
            before = jnp.dot(own_b, tri, preferred_element_type=f32) + running
            rank = jnp.sum(before * own, axis=0, keepdims=True).astype(jnp.int32)
            running = running + jnp.sum(own, axis=1, keepdims=True)
            at_rank = (
                (lax.broadcasted_iota(jnp.int32, (bucket, samples), 0) == rank)
                .astype(f32)
                .astype(bf16)
            )
            enc = enc_ref[t, l : l + 1, :].astype(f32)
            info_t += lax.dot_general(
                at_rank, (own * enc).astype(bf16), NT_DIMS, preferred_element_type=f32
            )
            high += lax.dot_general(
                (own * hi.astype(f32)).astype(bf16), at_rank, NT_DIMS, preferred_element_type=f32
            )
            low += lax.dot_general(
                (own * lo.astype(f32)).astype(bf16), at_rank, NT_DIMS, preferred_element_type=f32
            )
        rows_ref[:, t, :] = (high * DIGIT + low).astype(jnp.int32)
        info_i = info_t.astype(jnp.int32)
        lane = lax.broadcasted_iota(jnp.int32, (bucket, samples), 1)
        group = min(peers, 8)
        for g in range(0, peers, group):
            pick = jnp.concatenate(
                [
                    (lane == info_i[:, o : o + 1]).astype(f32).astype(bf16)
                    for o in range(g, g + group)
                ],
                axis=0,
            )
            moved = jnp.dot(pick, scaled_ref[t], preferred_element_type=f32).astype(bf16)
            terms_ref[t, g : g + group] = moved.reshape(group, bucket, moved.shape[1])


def exchange_kernel(
    n, inverse, terms_ref, rows_ref, summed_ref, scale_ref,
    got, got_rows, squares, got_squares, send, recv, local,
):
    f32, bf16 = jnp.float32, jnp.bfloat16
    count_tables, parts, part_rows, width = summed_ref.shape
    bucket = rows_ref.shape[2]
    count = n * bucket
    me = lax.axis_index("shard")
    barrier = pltpu.get_barrier_semaphore()

    @pl.loop(1, n)
    def _(i):
        pl.semaphore_signal(
            barrier, inc=1, device_id=(lax.rem(me + i, n),), device_id_type=MESH
        )

    own = [
        pltpu.make_async_copy(terms_ref.at[t, me], got.at[t, 0], local.at[t])
        for t in range(count_tables)
    ]
    own.append(pltpu.make_async_copy(rows_ref.at[me], got_rows.at[0], local.at[count_tables]))
    for copy in own:
        copy.start()
    pl.semaphore_wait(barrier, n - 1)

    def start(source, target, i, k):
        pltpu.make_async_remote_copy(
            src_ref=source,
            dst_ref=target,
            send_sem=send.at[k],
            recv_sem=recv.at[k],
            device_id=(lax.rem(me + i, n),),
            device_id_type=MESH,
        ).start()

    def drain(target, sem):
        others = target.at[pl.ds(1, n - 1)]
        pltpu.make_async_copy(others, others, sem).wait()

    @pl.loop(1, n)
    def _(i):
        start(rows_ref.at[lax.rem(me + i, n)], got_rows.at[i], i, count_tables)

    for t in range(count_tables):

        @pl.loop(1, n)
        def _(i):
            start(terms_ref.at[t, lax.rem(me + i, n)], got.at[t, i], i, t)

    own[-1].wait()
    drain(got_rows, recv.at[count_tables])
    chunk = min(512, part_rows)
    total = jnp.zeros((8, width), f32)
    for t in range(count_tables):
        rows = jnp.concatenate([got_rows[i, t : t + 1, :] for i in range(n)], axis=1)
        part = rows // part_rows
        within = rows - part * part_rows
        part_f = part.astype(f32)
        part_col = jnp.concatenate(
            [
                jnp.broadcast_to(part_f[:, c : c + 128], (128, 128)).T
                for c in range(0, count, 128)
            ],
            axis=0,
        )
        own[t].wait()
        drain(got.at[t], recv.at[t])
        terms = got[t].reshape(count, width).astype(f32)
        wide = jnp.concatenate(
            [jnp.where(part_col == q, terms, 0.0).astype(bf16) for q in range(parts)], axis=1
        )
        for m in range(0, part_rows, chunk):
            hot = (
                (lax.broadcasted_iota(jnp.int32, (chunk, count), 0) + m == within)
                .astype(f32)
                .astype(bf16)
            )
            summed = jnp.dot(hot, wide, preferred_element_type=f32)
            for q in range(parts):
                s = summed[:, q * width : (q + 1) * width]
                summed_ref[t, q, m : m + chunk, :] = s
                total += jnp.sum((s * s).reshape(chunk // 8, 8, width), axis=0)
    squares[...] = total
    for t in range(count_tables):
        drain(got.at[t], send.at[t])
    drain(got_rows, send.at[count_tables])

    @pl.loop(1, n)
    def _(i):
        start(squares, got_squares.at[i], i, count_tables + 1)

    drain(got_squares, recv.at[count_tables + 1])
    total = squares[...] + jnp.sum(got_squares[1:], axis=0)
    value = jnp.sum(jnp.sum(total, axis=1, keepdims=True), axis=0, keepdims=True)
    scale_ref[...] = jnp.broadcast_to(jnp.sqrt(value * inverse), scale_ref.shape)
    drain(got_squares, send.at[count_tables + 1])


def update_kernel(summed_ref, tables_ref, accum_ref, new_t_ref, new_a_ref):
    parts, part_rows, width = tables_ref.shape[1:]
    table, part = pl.program_id(0), pl.program_id(1)
    for q in range(parts):
        for r in range(0, part_rows, 128):
            s = summed_ref[table, part, r : r + 128, :]
            mean = jnp.sum((s * s).T, axis=0, keepdims=True) * (1.0 / width)
            line = r // 128
            new_a = accum_ref[0, q, line : line + 1, :] + mean
            new_a_ref[0, q, line : line + 1, :] = new_a
            factor = step_size / (jnp.sqrt(new_a) + epsilon)
            spread = jnp.broadcast_to(factor, (128, 128)).T
            new_t_ref[0, q, r : r + 128, :] = tables_ref[0, q, r : r + 128, :] - s * spread


def on_device(lookup_ids, bag_lengths, pooled_gradients, tables, accumulators):
    samples, count_tables, bag_width = lookup_ids.shape
    width = pooled_gradients.shape[2]
    rows_dev = tables.shape[1]
    n = lax.axis_size("shard")
    lookups = samples * bag_width
    bucket = lookups // n
    vmem = pl.BlockSpec(memory_space=pltpu.VMEM)
    assert samples <= 256 and rows_dev <= 256 * DIGIT

    ids = lookup_ids.transpose(1, 2, 0)
    position = jnp.arange(bag_width, dtype=jnp.int32)
    sample = jnp.arange(samples, dtype=jnp.int32)
    inside = position[None, :, None] < bag_lengths.T[:, None, :]
    enc = jnp.where(inside, sample[None, None, :], -1)
    scaled = (
        (pooled_gradients.astype(jnp.float32) / bag_lengths[:, :, None].astype(jnp.float32))
        .astype(jnp.bfloat16)
        .transpose(1, 0, 2)
    )
    send_terms, send_rows = pl.pallas_call(
        functools.partial(arrange_kernel, n, bucket, rows_dev),
        out_shape=(
            jax.ShapeDtypeStruct((count_tables, n, bucket, width), jnp.bfloat16),
            jax.ShapeDtypeStruct((n, count_tables, bucket), jnp.int32),
        ),
        in_specs=[vmem] * 3,
        out_specs=(vmem, vmem),
        compiler_params=pltpu.CompilerParams(vmem_limit_bytes=16 * 1024 * 1024),
    )(ids, enc, scaled)

    parts = 4
    part_rows = rows_dev // parts
    lines = part_rows // 128
    lookup_count = width * count_tables * lookups * n
    dma = pltpu.SemaphoreType.DMA
    summed, scale = pl.pallas_call(
        functools.partial(exchange_kernel, n, 1.0 / lookup_count),
        out_shape=(
            jax.ShapeDtypeStruct((count_tables, parts, part_rows, width), jnp.float32),
            jax.ShapeDtypeStruct((8, 128), jnp.float32),
        ),
        in_specs=[vmem, vmem],
        out_specs=(vmem, vmem),
        scratch_shapes=[
            pltpu.VMEM((count_tables, n, bucket, width), jnp.bfloat16),
            pltpu.VMEM((n, count_tables, bucket), jnp.int32),
            pltpu.VMEM((8, width), jnp.float32),
            pltpu.VMEM((n, 8, width), jnp.float32),
            dma((count_tables + 2,)),
            dma((count_tables + 2,)),
            dma((count_tables + 1,)),
        ],
        compiler_params=pltpu.CompilerParams(
            collective_id=0, has_side_effects=True, vmem_limit_bytes=24 * 1024 * 1024
        ),
        cost_estimate=pl.CostEstimate(
            flops=2 * count_tables * lookups * rows_dev * width,
            bytes_accessed=32 * count_tables * lookups * width * 2,
            transcendentals=0,
        ),
    )(send_terms, send_rows)

    block = pl.BlockSpec((1, 1, part_rows, width), lambda t, q: (t, q, 0, 0))
    line_block = pl.BlockSpec((1, 1, lines, 128), lambda t, q: (t, q, 0, 0))
    new_tables, new_accumulators = pl.pallas_call(
        update_kernel,
        grid=(count_tables, parts),
        out_shape=(
            jax.ShapeDtypeStruct((count_tables, parts, part_rows, width), jnp.float32),
            jax.ShapeDtypeStruct((count_tables, parts, lines, 128), jnp.float32),
        ),
        in_specs=[vmem, block, line_block],
        out_specs=(block, line_block),
        compiler_params=pltpu.CompilerParams(vmem_limit_bytes=12 * 1024 * 1024),
    )(
        summed,
        tables.reshape(count_tables, parts, part_rows, width),
        accumulators.reshape(count_tables, parts, lines, 128),
    )
    return (
        new_tables.reshape(tables.shape),
        new_accumulators.reshape(accumulators.shape),
        scale[0, 0],
    )


def solution(mesh):
    return jax.shard_map(
        on_device,
        mesh=mesh,
        in_specs=(
            P("shard", None, None),
            P("shard", None),
            P("shard", None, None),
            P(None, "shard", None),
            P(None, "shard"),
        ),
        out_specs=(P(None, "shard", None), P(None, "shard"), P()),
        check_vma=False,
    )
```

time: 107 us -> 89.3 us (0.83)
  Pallas kernels: 96.6 us -> 82.9 us
  local copies, waits for them, and re-layouts: 5.25 us -> 2.79 us
  other arithmetic: 3.84 us -> 2.54 us
    pallas_call x3 -> x2, Pallas kernels: 86.6 us -> 75.2 us  [the longest x1 64.2 us: on_device(): pl.pallas_call(functools.partial(exchange_kernel, n, 1.0 / lookup_count),...]
    pallas_call x1, Pallas kernels: 10 us -> 7.71 us  [on_device(): pl.pallas_call(functools.partial(arrange_kernel, n, bucket, rows_dev), ou...]
    unnamed x6 -> x8, local copies, waits for them, and re-layouts: 3.1 us -> 2.28 us
where the time goes in v1:
time: 89.3 us; the launch traced here: 88.9 us
  Pallas kernels  82.9 us (93%)
  local copies, waits for them, and re-layouts  2.79 us (3%)
  other arithmetic  2.54 us (3%)
    pallas_call x1, Pallas kernels, on_device(): pl.pallas_call(functools.partial(exchange_kernel, n, 1.0 / lookup_count),...  64.2 us
    pallas_call x1, Pallas kernels, on_device(): pl.pallas_call(update_kernel, grid=(count_tables, parts), out_shape=(jax....  11.1 us
    pallas_call x1, Pallas kernels, on_device(): pl.pallas_call(functools.partial(arrange_kernel, n, bucket, rows_dev), ou...  7.71 us
    unnamed x8, local copies, waits for them, and re-layouts  2.28 us

profile of v1, /device:TPU:0, one launch (start us, length us, event | category | flops | bytes accessed | tf_op | source)
XLA Modules:
  0.0 88.9 jit_solution(16870306252846566601)
XLA Ops:
  0.6 0.7 convert_element_type.11
  1.3 0.7 iota_select_fusion.enc_ref
  2.0 0.8 copy.15
  2.9 1.2 %fusion.scaled_ref = bf16[4,256,128]{2,1,0:T(8,128)(2,1)S(1)} fusion(bf16[256,4,128]{2,1,0:T(4,128)(2,1)} %param.7, f32[256,4]{0,1:T(4,128)S(1)} %convert_element_type.11), kind=kLoop, calls=%fused_computation.1 | loop fusion | flops 393216 | bytes 528384 | tf_op jit(solution)/shard_map/transpose | solution.py:203
  4.0 0.0 copy-start
  4.0 0.7 copy-done
  4.8 0.0 slice-start
  4.8 7.7 %shard_map.76 = (bf16[4,32,64,128]{3,2,1,0:T(8,128)(2,1)S(1)}, s32[32,4,64]{2,1,0:T(4,128)S(1)}) custom-call(s32[4,8,256]{2,1,0:T(8,128)S(1)} %bitcast.22, s32[4,8,256]{2,1,0:T(8,128)S(1)} %iota_select_fusion.enc_ref, bf16[4,256,128]{2,1,0:T(8,128)(2,1)S(1)} %fusion.scaled_ref), custom_call_target="tpu_custom_call" | custom-call | tf_op jit(solution)/shard_map/pallas_call | solution.py:205
  12.5 0.0 slice-start.1
  12.5 64.2 %shard_map.77 = (f32[4,4,1024,128]{3,2,1,0:T(8,128)S(1)}, f32[8,128]{1,0:T(8,128)S(1)}) custom-call(bf16[4,32,64,128]{3,2,1,0:T(8,128)(2,1)S(1)} %get-tuple-element.9.terms_ref, s32[32,4,64]{2,1,0:T(4,128)S(1)} %get-tuple-element.10.rows_ref), custom_call_target="tpu_custom_call" | custom-call | flops 8589934592 | bytes 67108864 | tf_op jit(solution)/shard_map/pallas_call | solution.py:221
  76.7 0.5 slice.3
  77.2 0.0 slice-done
  77.2 0.0 slice-done.1
  77.2 11.1 %shard_map.78 = (f32[4,4,1024,128]{3,2,1,0:T(8,128)}, f32[4,4,8,128]{3,2,1,0:T(8,128)S(1)}) custom-call(f32[4,4,1024,128]{3,2,1,0:T(8,128)S(1)} %get-tuple-element.11.summed_ref, f32[4,4,1024,128]{3,2,1,0:T(8,128)S(1)} %bitcast.19, f32[4,4,8,128]{3,2,1,0:T(8,128)S(1)} %bitcast.20), custom_call_target="tpu_custom_call" | custom-call | tf_op jit(solution)/shard_map/pallas_call | solution.py:250
  88.3 0.7 copy.14
  (1 shorter events, 0.0 us)
Async XLA Ops:
  4.0 0.8 copy-start
  4.8 72.4 %slice-start = ((s8[8388608]{0:T(1024)(128)(4,1)}), s8[4194304]{0:T(1024)(128)(4,1)S(1)}, s32[]{:S(2)}) async-start(s8[8388608]{0:T(1024)(128)(4,1)} %bitcast.17), calls=%async_computation | async-start | bytes 8388608
  12.5 64.7 %slice-start.1 = ((s8[8388608]{0:T(1024)(128)(4,1)}), s8[4194304]{0:T(1024)(128)(4,1)S(1)}, s32[]{:S(2)}) async-start(s8[8388608]{0:T(1024)(128)(4,1)} %bitcast.17), calls=%async_computation.1 | async-start | bytes 8388608
